TPU v7x, 512 devices: a whole 4x8x8 slice. The times are simulated.
512 devices in a mesh: unit: 2 (over y_1), row: 16 (over y_0, x, core), col: 16 (over z, y_2).
Axes of the slice: x: 4, y: 8 (y_0: 2, y_1: 2, y_2: 2; y = y_0 * 4 + y_1 * 2 + y_2), z: 8, core: 2. Of those that a mesh axis runs over, the one named last changes fastest.
Arguments:
- tracer: float32 [4, 128, 256, 256], P('unit', None, 'row', 'col'), parts along dimension 0, may hold values from -6 to 6
- symbol_x: float32 [128], replicated, may hold values from 0.3 to 3
- symbol_y: float32 [256], replicated, may hold values from 0.3 to 3
- symbol_z: float32 [256], replicated, may hold values from 0.3 to 3
Outputs:
- smoothed: float32 [4, 128, 256, 256], P('unit', None, 'row', 'col'), parts along dimension 0
There are 2 independent parts, one for each index of `unit`. A program takes and returns all parts, laid end to end along the dimension named above; an argument that names none is the same for every part. Nothing has to cross between parts.
All inputs are finite; a program needn't handle non-finite values.
Results may differ from a plain program's by a relative error of at most 0.0003.
Values sent between devices are 32-bit elements.
A program may use at most 64 MiB of HBM per device.

v0:
```python
import jax
import jax.numpy as jnp
from jax import lax
from jax.sharding import PartitionSpec as P


def mode_table(count):
    rank = jnp.arange(count)
    angle = (
        jnp.pi
        / (4 * count)
        * ((2 * rank[:, None] + 1) * (2 * rank[None, :] + 1) % (8 * count)).astype(jnp.float32)
    )
    return jnp.cos(angle) * (2.0 / count) ** 0.5


def to_modes(values, dim):
    moved = jnp.tensordot(
        values, mode_table(values.shape[dim]), axes=([dim], [0]), precision=lax.Precision.HIGHEST
    )
    return jnp.moveaxis(moved, -1, dim)


def shards(tracer, symbol_x, symbol_y, symbol_z):

    def forward_part(part_values):
        part_values = to_modes(part_values, 1)
        part_values = lax.all_to_all(part_values, "row", split_axis=1, concat_axis=2, tiled=True)
        part_values = to_modes(part_values, 2)
        part_values = lax.all_to_all(part_values, "col", split_axis=2, concat_axis=3, tiled=True)
        return to_modes(part_values, 3)

    def backward_part(part_values):
        part_values = to_modes(part_values, 3)
        part_values = lax.all_to_all(part_values, "col", split_axis=3, concat_axis=2, tiled=True)
        part_values = to_modes(part_values, 2)
        part_values = lax.all_to_all(part_values, "row", split_axis=2, concat_axis=1, tiled=True)
        return to_modes(part_values, 1)

    block_values = forward_part(tracer)
    share_x = block_values.shape[1]
    part_x = lax.dynamic_slice_in_dim(symbol_x, lax.axis_index("row") * share_x, share_x)
    share_y = block_values.shape[2]
    part_y = lax.dynamic_slice_in_dim(symbol_y, lax.axis_index("col") * share_y, share_y)
    symbol = part_x[:, None, None] + part_y[None, :, None] + symbol_z[None, None, :]
    block_values = block_values * lax.rsqrt(symbol)
    block_values = backward_part(block_values)
    return block_values


def solution(mesh):
    in_specs = (P("unit", None, "row", "col"), P(), P(), P())
    out_specs = P("unit", None, "row", "col")
    return jax.shard_map(shards, mesh=mesh, in_specs=in_specs, out_specs=out_specs, check_vma=False)
```

profile of v0, /device:TPU:8, one launch (start us, length us, event | category | flops | bytes accessed | tf_op | source)
XLA Modules:
  0.0 125.6 jit_solution(17801068232473638482)
XLA Ops:
  0.0 0.0 copy-start
  0.0 0.9 copy-done
  1.0 0.7 fusion.51
  1.6 1.8 %copy.14 = f32[2,128,16,16]{3,2,0,1:T(8,128)S(1)} copy(f32[2,128,16,16]{1,3,2,0:T(8,128)S(1)} %bitcast.75) | data formatting | bytes 524288 | tf_op jit(solution)/shard_map/transpose | solution.py:21
  3.5 1.5 %reshape.67 = f32[16,1,4096]{2,1,0:T(1,128)} reshape(f32[128,2,16,16]{3,2,1,0:T(8,128)S(1)} %bitcast.64) | data formatting | bytes 524288
  4.9 8.8 %all-to-all-start = ((f32[16,1,4096]{2,1,0:T(1,128)}), f32[16,1,4096]{2,1,0:T(1,128)S(1)}, u32[]{:S(2)}, u32[]{:S(2)}) async-start(f32[16,1,4096]{2,1,0:T(1,128)} %reshape.67), calls=%async_computation | async-start | bytes 524288 | tf_op jit(solution)/shard_map/all_to_all | solution.py:28
  13.7 15.1 %all-to-all-done = f32[16,1,4096]{2,1,0:T(1,128)S(1)} async-done(((f32[16,1,4096]{2,1,0:T(1,128)}), f32[16,1,4096]{2,1,0:T(1,128)S(1)}, u32[]{:S(2)}, u32[]{:S(2)}) %all-to-all-start) | async-done | bytes 262176 | tf_op jit(solution)/shard_map/all_to_all | solution.py:28
  28.9 0.5 broadcast.193
  29.4 1.2 reduce
  30.6 0.7 reshape.68
  31.3 2.0 %copy.16 = f32[2,8,16,16,16]{3,2,4,1,0:T(8,128)} copy(f32[2,8,16,16,16]{4,3,0,1,2:T(8,128)S(1)} %bitcast.69) | data formatting | bytes 524288 | tf_op jit(solution)/shard_map/all_to_all | solution.py:28
  33.4 2.4 %all_to_all.55 = f32[2,8,256,16]{2,3,1,0:T(8,128)S(1)} reshape(f32[2,8,16,16,16]{3,2,4,1,0:T(8,128)} %copy.16) | data formatting | bytes 524288 | tf_op jit(solution)/shard_map/all_to_all | solution.py:28
  35.8 1.4 %convolution_bitcast_fusion.1 = f32[2,8,256,16]{2,3,1,0:T(8,128)S(1)} fusion(f32[2,8,256,16]{2,3,1,0:T(8,128)S(1)} %all_to_all.55, s32[256]{0:T(256)S(1)} %multiply_add_fusion), kind=kOutput, calls=%fused_computation.6 | convolution fusion | flops 202309632 | bytes 525312 | tf_op jit(solution)/shard_map/dot_general | solution.py:18
  37.3 0.0 copy-start.2
  37.3 0.0 copy-start.3
  37.3 0.0 copy-start.1
  37.3 1.3 %copy.17 = f32[2,8,256,16]{3,1,0,2:T(8,128)S(1)} copy(f32[2,8,256,16]{2,3,1,0:T(8,128)S(1)} %convolution_bitcast_fusion.1) | data formatting | bytes 524288 | tf_op jit(solution)/shard_map/transpose | solution.py:21
  38.6 1.5 %reshape.69 = f32[16,1,4096]{2,1,0:T(1,128)} reshape(f32[256,2,8,16]{3,2,1,0:T(8,128)S(1)} %bitcast.65) | data formatting | bytes 524288
  40.0 11.8 %all-to-all-start.1 = ((f32[16,1,4096]{2,1,0:T(1,128)}), f32[16,1,4096]{2,1,0:T(1,128)S(1)}, u32[]{:S(2)}, u32[]{:S(2)}) async-start(f32[16,1,4096]{2,1,0:T(1,128)} %reshape.69), calls=%async_computation.1 | async-start | bytes 524288 | tf_op jit(solution)/shard_map/all_to_all | solution.py:30
  51.8 0.0 copy-done.2
  51.8 0.1 dynamic_slice.7
  51.9 0.0 copy-done.3
  51.9 0.1 dynamic_slice.6
  52.0 0.1 broadcast_add_fusion
  52.1 0.0 copy-done.1
  52.1 0.1 add_rsqrt_fusion
  52.2 10.2 %all-to-all-done.1 = f32[16,1,4096]{2,1,0:T(1,128)S(1)} async-done(((f32[16,1,4096]{2,1,0:T(1,128)}), f32[16,1,4096]{2,1,0:T(1,128)S(1)}, u32[]{:S(2)}, u32[]{:S(2)}) %all-to-all-start.1) | async-done | bytes 262176 | tf_op jit(solution)/shard_map/all_to_all | solution.py:30
  62.4 1.2 reduce.1
  63.6 0.7 reshape.70
  64.3 2.6 %copy.34 = f32[2,8,16,16,16]{4,2,3,1,0:T(8,128)} copy(f32[2,8,16,16,16]{4,1,0,3,2:T(8,128)S(1)} %bitcast.70) | data formatting | bytes 524288 | tf_op jit(solution)/shard_map/all_to_all | solution.py:30
  66.9 2.4 %all_to_all.59 = f32[2,8,16,256]{3,2,1,0:T(8,128)S(1)} reshape(f32[2,8,16,16,16]{4,3,2,1,0:T(8,128)} %bitcast.71) | data formatting | bytes 524288 | tf_op jit(solution)/shard_map/all_to_all | solution.py:30
  69.3 1.4 %convolution_multiply_fusion = f32[2,8,16,256]{3,2,1,0:T(8,128)S(1)} fusion(f32[2,8,16,256]{3,2,1,0:T(8,128)S(1)} %all_to_all.59, f32[8,16,256]{2,1,0:T(8,128)S(1)} %add_rsqrt_fusion, s32[256]{0:T(256)S(1)} %multiply_add_fusion), kind=kOutput, calls=%fused_computation.5 | convolution fusion | flops 202375168 | bytes 656384 | tf_op jit(solution)/shard_map/dot_general | solution.py:18
  70.8 1.4 %fusion.12 = f32[2,8,16,256]{3,2,1,0:T(8,128)S(1)} fusion(f32[2,8,16,256]{3,2,1,0:T(8,128)S(1)} %convolution_multiply_fusion, s32[256]{0:T(256)S(1)} %multiply_add_fusion), kind=kOutput, calls=%fused_computation.19 | convolution fusion | flops 202309632 | bytes 525312 | tf_op jit(solution)/shard_map/dot_general | solution.py:18
  72.2 1.3 %copy.19 = f32[2,8,16,256]{2,1,0,3:T(8,128)S(1)} copy(f32[2,8,16,256]{3,2,1,0:T(8,128)S(1)} %fusion.12) | data formatting | bytes 524288 | tf_op jit(solution)/shard_map/dot_general | solution.py:18
  73.5 0.7 reshape.71
  74.2 14.5 %all_to_all.72 = f32[16,1,4096]{2,1,0:T(1,128)S(1)} all-to-all(f32[16,1,4096]{2,1,0:T(1,128)S(1)} %reshape.71), channel_id=1, replica_groups=mesh['unit'=2,'row'=16,'col'=16] {'col'}, dimensions={0} | all-to-all | bytes 524288 | tf_op jit(solution)/shard_map/all_to_all | solution.py:35
  88.7 1.2 reduce.2
  89.9 0.7 reshape.72
  90.6 2.6 %copy.33 = f32[2,8,16,16,16]{2,3,4,1,0:T(8,128)} copy(f32[2,8,16,16,16]{2,1,0,4,3:T(8,128)S(1)} %bitcast.72) | data formatting | bytes 524288 | tf_op jit(solution)/shard_map/all_to_all | solution.py:35
  93.2 2.4 %all_to_all.63 = f32[2,8,256,16]{2,3,1,0:T(8,128)S(1)} reshape(f32[2,8,16,16,16]{3,2,4,1,0:T(8,128)} %bitcast.73) | data formatting | bytes 524288 | tf_op jit(solution)/shard_map/all_to_all | solution.py:35
  95.7 1.4 %convolution_bitcast_fusion = f32[2,8,256,16]{2,3,1,0:T(8,128)S(1)} fusion(f32[2,8,256,16]{2,3,1,0:T(8,128)S(1)} %all_to_all.63, s32[256]{0:T(256)S(1)} %multiply_add_fusion), kind=kOutput, calls=%fused_computation.4 | convolution fusion | flops 202309632 | bytes 525312 | tf_op jit(solution)/shard_map/dot_general | solution.py:18
  97.1 1.3 %copy.21 = f32[2,8,256,16]{3,1,0,2:T(8,128)S(1)} copy(f32[2,8,256,16]{2,3,1,0:T(8,128)S(1)} %convolution_bitcast_fusion) | data formatting | bytes 524288 | tf_op jit(solution)/shard_map/transpose | solution.py:21
  98.4 0.7 reshape.73
  99.1 19.3 %all_to_all.73 = f32[16,1,4096]{2,1,0:T(1,128)S(1)} all-to-all(f32[16,1,4096]{2,1,0:T(1,128)S(1)} %reshape.73), channel_id=1, replica_groups=mesh['unit'=2,'row'=16,'col'=16] {'row'}, dimensions={0} | all-to-all | bytes 524288 | tf_op jit(solution)/shard_map/all_to_all | solution.py:37
  118.4 1.2 reduce.3
  119.7 0.7 reshape.74
  120.4 0.7 copy.22
  121.1 4.5 %fusion.2 = f32[2,128,16,16]{1,3,2,0:T(8,128)} fusion(f32[2,128,16,16]{3,2,1,0:T(8,128)S(1)} %bitcast.68, s32[128]{0:T(128)S(1)} %multiply_add_fusion.1), kind=kOutput, calls=%fused_computation.7 | convolution fusion | flops 100909056 | bytes 524800 | tf_op jit(solution)/shard_map/dot_general | solution.py:18
  (2 shorter events, 0.0 us)
Async XLA Ops:
  0.0 1.0 copy-start
  4.9 23.9 %all-to-all-start = ((f32[16,1,4096]{2,1,0:T(1,128)}), f32[16,1,4096]{2,1,0:T(1,128)S(1)}, u32[]{:S(2)}, u32[]{:S(2)}) async-start(f32[16,1,4096]{2,1,0:T(1,128)} %reshape.67), calls=%async_computation | async-start | bytes 524288 | tf_op jit(solution)/shard_map/all_to_all | solution.py:28
  37.3 14.6 %copy-start.2 = (f32[256]{0:T(256)S(1)}, f32[256]{0:T(256)}, u32[]{:S(2)}) copy-start(f32[256]{0:T(256)} %param.6) | copy-start | bytes 3076
  37.3 14.7 %copy-start.3 = (f32[128]{0:T(128)S(1)}, f32[128]{0:T(128)}, u32[]{:S(2)}) copy-start(f32[128]{0:T(128)} %param.5) | copy-start | bytes 1540
  37.3 14.8 %copy-start.1 = (f32[256]{0:T(256)S(1)}, f32[256]{0:T(256)}, u32[]{:S(2)}) copy-start(f32[256]{0:T(256)} %param.7) | copy-start | bytes 3076
  40.0 22.3 %all-to-all-start.1 = ((f32[16,1,4096]{2,1,0:T(1,128)}), f32[16,1,4096]{2,1,0:T(1,128)S(1)}, u32[]{:S(2)}, u32[]{:S(2)}) async-start(f32[16,1,4096]{2,1,0:T(1,128)} %reshape.69), calls=%async_computation.1 | async-start | bytes 524288 | tf_op jit(solution)/shard_map/all_to_all | solution.py:30
where the time goes:
time: 126 us
  blocking collectives  33.8 us (27%)
  local copies, waits for them, and re-layouts  29.7 us (24%)
  waiting for transfers between devices  25.4 us (20%)
  starting transfers between devices  20.6 us (16%)
  matrix products  10.8 us (9%)
  other arithmetic  5.09 us (4%)
    all_to_all x1, blocking collectives, backward_part(): lax.all_to_all(part_values, 'row', split_axis=2, concat_axis=1, tiled=True)  19.3 us
    all_to_all x1, waiting for transfers between devices, forward_part(): lax.all_to_all(part_values, 'row', split_axis=1, concat_axis=2, tiled=True)  15.1 us
    all_to_all x1, blocking collectives, backward_part(): lax.all_to_all(part_values, 'col', split_axis=3, concat_axis=2, tiled=True)  14.5 us
    all_to_all x1, starting transfers between devices, forward_part(): lax.all_to_all(part_values, 'col', split_axis=2, concat_axis=3, tiled=True)  11.8 us
    all_to_all x1, waiting for transfers between devices, forward_part(): lax.all_to_all(part_values, 'col', split_axis=2, concat_axis=3, tiled=True)  10.2 us
    dot_general x5, matrix products, to_modes(): jnp.tensordot(values, mode_table(values.shape[dim]), axes=([dim], [0]), p...  10.1 us
    all_to_all x1, starting transfers between devices, forward_part(): lax.all_to_all(part_values, 'row', split_axis=1, concat_axis=2, tiled=True)  8.77 us
    unnamed x16, local copies, waits for them, and re-layouts  8.21 us
  transfers between devices with their start and end apart: 2, of which 2 were waited for; matrix products, arithmetic and copies ran while one was open for 0% of the time, Pallas kernels for 0%

commit v1 on v0

v1 whole, which is shorter than its diff:
```python
import functools

import jax
import jax.numpy as jnp
import numpy as np
from jax import lax
from jax.experimental import pallas as pl
from jax.experimental.pallas import tpu as pltpu
from jax.sharding import PartitionSpec as P

MESH = pl.DeviceIdType.MESH
F32, BF16 = jnp.float32, jnp.bfloat16


def mode_table(count):
    rank = np.arange(count)
    angle = np.pi / (4 * count) * ((2 * rank[:, None] + 1) * (2 * rank[None, :] + 1) % (8 * count))
    table = (np.cos(angle) * np.sqrt(2.0 / count)).astype(np.float32)
    high = table.astype(jnp.bfloat16)
    low = (table - high.astype(np.float32)).astype(jnp.bfloat16)
    return np.stack([high, low])


def split(values):
    high = values.astype(BF16)
    return high, (values - high.astype(F32)).astype(BF16)


def dot(a, b, dims):
    out = None
    for i, j in ((0, 1), (1, 0), (0, 0)):
        term = lax.dot_general(a[i], b[j], (dims, ((), ())), preferred_element_type=F32)
        out = term if out is None else out + term
    return out


NN, NT, TN = ((1,), (0,)), ((1,), (1,)), ((0,), (0,))


def exchanged(tiles):
    tiles = pltpu.roll(tiles, 0, 2, stride=16, stride_axis=1)
    group = lax.broadcasted_iota(jnp.int32, tiles.shape, 2) // 16
    for bit, step in ((1, 7), (2, 6), (4, 4)):
        tiles = jnp.where(group // bit % 2 == 1, pltpu.roll(tiles, step, 1), tiles)
    return pltpu.roll(tiles, 0, 2, stride=16, stride_axis=1)


def kernel(a_ref, hx_ref, h_ref, hb_ref, sx_ref, sy_ref, sz_ref, out_ref,
           send1, recv1, recv2, send3, recv3, recv4, send_sem, recv_sem, own_sem):
    r, c = lax.axis_index("row"), lax.axis_index("col")
    barrier = pltpu.get_barrier_semaphore()

    @pl.loop(1, 16)
    def _(i):
        pl.semaphore_signal(barrier, inc=1, device_id={"row": (r + i) % 16}, device_id_type=MESH)
        pl.semaphore_signal(barrier, inc=1, device_id={"col": (c + i) % 16}, device_id_type=MESH)

    def slot(col):
        return col // 8 * 8 + (8 - col % 8) % 8

    def refs(k, h, mine, t):
        if k == 0:
            return send1.at[h, t], recv1.at[h, mine]
        if k == 1:
            return recv1.at[h, :, pl.ds(t, 1)], recv2.at[h, :, pl.ds(mine, 1)]
        if k == 2:
            return send3.at[h, :, pl.ds(slot(t), 1)], recv3.at[h, :, pl.ds(mine, 1)]
        return recv3.at[h, t], recv4.at[h, mine]

    def start(k, h):
        axis, mine = ("row", r) if k in (0, 3) else ("col", c)

        @pl.loop(1, 16)
        def _(i):
            t = (mine + i) % 16
            src, dst = refs(k, h, mine, t)
            pltpu.make_async_remote_copy(src, dst, send_sem.at[k, h], recv_sem.at[k, h],
                                         device_id={axis: t}, device_id_type=MESH).start()
        src, dst = refs(k, h, mine, mine)
        pltpu.make_async_copy(src, dst, own_sem.at[k, h]).start()

    def finish(k, h):
        axis, mine = ("row", r) if k in (0, 3) else ("col", c)
        src, dst = refs(k, h, mine, mine)
        pltpu.make_async_copy(src, dst, own_sem.at[k, h]).wait()
        part = send1.at[h, pl.ds(0, 15)]
        pltpu.make_async_copy(part, part, recv_sem.at[k, h]).wait()

    def sent(k, h):
        part = send1.at[h, pl.ds(0, 15)]
        pltpu.make_async_copy(part, part, send_sem.at[k, h]).wait()

    hx = hx_ref[0], hx_ref[1]
    table = h_ref[0], h_ref[1]
    backwards = hb_ref[0], hb_ref[1]
    for f in range(2):
        for h in range(2):
            rows = split(a_ref[f, pl.ds(8 * h, 8)].reshape(128, 128))
            send1[h, pl.ds(8 * f, 8)] = dot(hx, rows, NT).reshape(8, 16, 128)
    pl.semaphore_wait(barrier, 30)
    for h in range(2):
        start(0, h)

    symbol_y = jnp.broadcast_to(sy_ref[...], (256, 256)).T
    symbol = sx_ref[r % 8 * 16 + c] + symbol_y + sz_ref[...]
    scale = lax.rsqrt(symbol)

    for h in range(2):
        finish(0, h)
        start(1, h)
    for h in range(2):
        finish(1, h)

    tiles = exchanged(recv2[...].reshape(64, 8, 128)).reshape(2, 16, 2, 8, 128)
    plane = jnp.concatenate(
        [jnp.stack([tiles[0, :, g], tiles[1, :, g]], axis=1).reshape(256, 128) for g in range(2)], axis=1
    )
    plane = dot(split(plane), table, NN)
    plane = dot(backwards, split(plane), NN) * scale
    plane = dot(table, split(plane), NN)
    plane = dot(split(plane), table, NN).reshape(16, 2, 8, 256)
    for h in range(2):
        part = jnp.stack([plane[:, h, :, :128], plane[:, h, :, 128:]], axis=1).reshape(32, 8, 128)
        send3[h] = exchanged(part).reshape(16, 16, 128)
        start(2, h)
    for h in range(2):
        finish(2, h)
        start(3, h)
    for h in range(2):
        finish(3, h)
        for f in range(2):
            rows = split(recv4[h, pl.ds(8 * f, 8)].reshape(128, 128))
            out_ref[f, pl.ds(8 * h, 8)] = dot(rows, hx, TN).reshape(8, 16, 128)
    for k in range(4):
        for h in range(2):
            sent(k, h)


def shards(tracer, symbol_x, symbol_y, symbol_z):
    values = jnp.transpose(tracer, (0, 2, 3, 1))
    vmem, smem = pl.BlockSpec(memory_space=pltpu.VMEM), pl.BlockSpec(memory_space=pltpu.SMEM)
    table, place = mode_table(256), np.arange(256)
    backwards = place // 8 * 8 + -place % 8
    block = pltpu.VMEM((2, 16, 16, 128), F32)
    out = pl.pallas_call(
        kernel,
        out_shape=jax.ShapeDtypeStruct(values.shape, F32),
        in_specs=[vmem, vmem, vmem, vmem, smem, vmem, vmem],
        out_specs=vmem,
        scratch_shapes=[block] * 6 + [pltpu.SemaphoreType.DMA((4, 2))] * 3,
        compiler_params=pltpu.CompilerParams(collective_id=0, has_side_effects=True),
    )(values, jnp.asarray(mode_table(128)), jnp.asarray(table), jnp.asarray(table[:, :, backwards]),
      symbol_x, symbol_y.reshape(1, 256), symbol_z.reshape(1, 256))
    return jnp.transpose(out, (0, 3, 1, 2))


def solution(mesh):
    in_specs = (P("unit", None, "row", "col"), P(), P(), P())
    out_specs = P("unit", None, "row", "col")
    return jax.shard_map(shards, mesh=mesh, in_specs=in_specs, out_specs=out_specs, check_vma=False)
```

time: 126 us -> 55.6 us (0.44)
  the two profiles are of different devices: /device:TPU:8 before, /device:TPU:1 now
where the time goes in v1:
time: 55.6 us; the launch traced here: 55.4 us
  Pallas kernels  53.7 us (97%)
  local copies, waits for them, and re-layouts  1.67 us (3%)
    pallas_call x1, Pallas kernels, shards(): pl.pallas_call(kernel, out_shape=jax.ShapeDtypeStruct(values.shape, F32),...  53.7 us
    unnamed x1, local copies, waits for them, and re-layouts  1.67 us

profile of v1, /device:TPU:1, one launch (start us, length us, event | category | flops | bytes accessed | tf_op | source)
XLA Modules:
  0.0 55.4 jit_solution(811718971201063313)
XLA Ops:
  0.0 53.7 %shard_map.73 = f32[2,16,16,128]{3,2,1,0:T(8,128)} custom-call(f32[2,16,16,128]{3,2,1,0:T(8,128)} %bitcast.5, bf16[2,128,128]{2,1,0:T(8,128)(2,1)} %constant.6.clone.hx_ref, bf16[2,256,256]{2,1,0:T(8,128)(2,1)} %constant.7.clone.h_ref, bf16[2,256,256]{2,1,0:T(8,128)(2,1)} %constant.8.clone.hb_ref, f32[128]{0:T(128)} %sx_ref.1, f32[1,256]{1,0:T(1,128)} %bitcast.6, ...), custom_call_target="tpu_custom_call" | custom-call | tf_op jit(solution)/shard_map/pallas_call | solution.py:145
  53.7 1.7 %copy.9 = f32[2,128,16,16]{1,3,2,0:T(8,128)} copy(f32[2,128,16,16]{1,3,2,0:T(8,128)} %bitcast.4) | data formatting | bytes 524288

commit v2 on v1

--- a/solution.py
+++ b/solution.py
@@ -9,6 +9,9 @@
 from jax.sharding import PartitionSpec as P
 
 MESH = pl.DeviceIdType.MESH
+OUT = (1, 0), (0, 0), (0, 1), (1, 1)
+OUT_NEXT = (0, 0), (0, 1), (1, 0), (1, 1)
+BACK = (1, 0), (1, 1), (0, 0), (0, 1)
 F32, BF16 = jnp.float32, jnp.bfloat16
 
 
@@ -58,37 +61,43 @@
     def slot(col):
         return col // 8 * 8 + (8 - col % 8) % 8
 
-    def refs(k, h, mine, t):
+    half = r // 8
+    near, far = half * 8, (1 - half) * 8
+
+    def refs(k, h, base, mine, t):
         if k == 0:
             return send1.at[h, t], recv1.at[h, mine]
         if k == 1:
-            return recv1.at[h, :, pl.ds(t, 1)], recv2.at[h, :, pl.ds(mine, 1)]
+            return recv1.at[h, pl.ds(base, 8), pl.ds(t, 1)], recv2.at[h, pl.ds(base, 8), pl.ds(mine, 1)]
         if k == 2:
-            return send3.at[h, :, pl.ds(slot(t), 1)], recv3.at[h, :, pl.ds(mine, 1)]
+            return send3.at[h, pl.ds(base, 8), pl.ds(slot(t), 1)], recv3.at[h, pl.ds(base, 8), pl.ds(mine, 1)]
         return recv3.at[h, t], recv4.at[h, mine]
 
-    def start(k, h):
-        axis, mine = ("row", r) if k in (0, 3) else ("col", c)
+    def own(k, h, side):
+        return pltpu.make_async_copy(*refs(k, h, (near, far)[side], *((r, r) if k in (0, 3) else (c, c))),
+                                     own_sem.at[k, side, h])
 
-        @pl.loop(1, 16)
+    def start(k, side, h):
+        base, rows = (near, far)[side], k in (0, 3)
+        axis, mine = ("row", r) if rows else ("col", c)
+
+        @pl.loop(0 if rows and side else 1, 8 if rows else 16)
         def _(i):
-            t = (mine + i) % 16
-            src, dst = refs(k, h, mine, t)
-            pltpu.make_async_remote_copy(src, dst, send_sem.at[k, h], recv_sem.at[k, h],
+            t = base + (r + i) % 8 if rows else (c + i) % 16
+            src, dst = refs(k, h, base, mine, t)
+            pltpu.make_async_remote_copy(src, dst, send_sem.at[k, side, h], recv_sem.at[k, side, h],
                                          device_id={axis: t}, device_id_type=MESH).start()
-        src, dst = refs(k, h, mine, mine)
-        pltpu.make_async_copy(src, dst, own_sem.at[k, h]).start()
+        if not (rows and side):
+            own(k, h, side).start()
 
-    def finish(k, h):
-        axis, mine = ("row", r) if k in (0, 3) else ("col", c)
-        src, dst = refs(k, h, mine, mine)
-        pltpu.make_async_copy(src, dst, own_sem.at[k, h]).wait()
-        part = send1.at[h, pl.ds(0, 15)]
-        pltpu.make_async_copy(part, part, recv_sem.at[k, h]).wait()
+    def await_all(k, side, h, sem):
+        part = send1.at[h, pl.ds(0, 7 + side)] if k in (0, 3) else send1.at[h, pl.ds(0, 15), pl.ds(0, 8)]
+        pltpu.make_async_copy(part, part, sem.at[k, side, h]).wait()
 
-    def sent(k, h):
-        part = send1.at[h, pl.ds(0, 15)]
-        pltpu.make_async_copy(part, part, send_sem.at[k, h]).wait()
+    def finish(k, side, h):
+        if k in (1, 2) or not side:
+            own(k, h, side).wait()
+        await_all(k, side, h, recv_sem)
 
     hx = hx_ref[0], hx_ref[1]
     table = h_ref[0], h_ref[1]
@@ -98,18 +107,18 @@
             rows = split(a_ref[f, pl.ds(8 * h, 8)].reshape(128, 128))
             send1[h, pl.ds(8 * f, 8)] = dot(hx, rows, NT).reshape(8, 16, 128)
     pl.semaphore_wait(barrier, 30)
-    for h in range(2):
-        start(0, h)
+    for side, h in OUT:
+        start(0, side, h)
 
     symbol_y = jnp.broadcast_to(sy_ref[...], (256, 256)).T
     symbol = sx_ref[r % 8 * 16 + c] + symbol_y + sz_ref[...]
     scale = lax.rsqrt(symbol)
 
-    for h in range(2):
-        finish(0, h)
-        start(1, h)
-    for h in range(2):
-        finish(1, h)
+    for side, h in OUT_NEXT:
+        finish(0, side, h)
+        start(1, side, h)
+    for side, h in OUT_NEXT:
+        finish(1, side, h)
 
     tiles = exchanged(recv2[...].reshape(64, 8, 128)).reshape(2, 16, 2, 8, 128)
     plane = jnp.concatenate(
@@ -122,18 +131,19 @@
     for h in range(2):
         part = jnp.stack([plane[:, h, :, :128], plane[:, h, :, 128:]], axis=1).reshape(32, 8, 128)
         send3[h] = exchanged(part).reshape(16, 16, 128)
-        start(2, h)
-    for h in range(2):
-        finish(2, h)
-        start(3, h)
-    for h in range(2):
-        finish(3, h)
-        for f in range(2):
-            rows = split(recv4[h, pl.ds(8 * f, 8)].reshape(128, 128))
-            out_ref[f, pl.ds(8 * h, 8)] = dot(rows, hx, TN).reshape(8, 16, 128)
+    for side, h in BACK:
+        start(2, side, h)
+    for side, h in BACK:
+        finish(2, side, h)
+        start(3, side, h)
+    for side, h in BACK:
+        finish(3, side, h)
+        f = (half, 1 - half)[side]
+        rows = split(recv4[h, pl.ds(8 * f, 8)].reshape(128, 128))
+        out_ref[f, pl.ds(8 * h, 8)] = dot(rows, hx, TN).reshape(8, 16, 128)
     for k in range(4):
-        for h in range(2):
-            sent(k, h)
+        for side, h in OUT:
+            await_all(k, side, h, send_sem)
 
 
 def shards(tracer, symbol_x, symbol_y, symbol_z):
@@ -147,7 +157,7 @@
         out_shape=jax.ShapeDtypeStruct(values.shape, F32),
         in_specs=[vmem, vmem, vmem, vmem, smem, vmem, vmem],
         out_specs=vmem,
-        scratch_shapes=[block] * 6 + [pltpu.SemaphoreType.DMA((4, 2))] * 3,
+        scratch_shapes=[block] * 6 + [pltpu.SemaphoreType.DMA((4, 2, 2))] * 3,
         compiler_params=pltpu.CompilerParams(collective_id=0, has_side_effects=True),
     )(values, jnp.asarray(mode_table(128)), jnp.asarray(table), jnp.asarray(table[:, :, backwards]),
       symbol_x, symbol_y.reshape(1, 256), symbol_z.reshape(1, 256))

time: 55.6 us -> 54.8 us (0.986)
  Pallas kernels: 53.7 us -> 53 us
    pallas_call x1, Pallas kernels: 53.7 us -> 53 us  [shards(): pl.pallas_call(kernel, out_shape=jax.ShapeDtypeStruct(values.shape, F32),...]
where the time goes in v2:
time: 54.8 us; the launch traced here: 54.7 us
  Pallas kernels  53 us (97%)
  local copies, waits for them, and re-layouts  1.67 us (3%)
    pallas_call x1, Pallas kernels, shards(): pl.pallas_call(kernel, out_shape=jax.ShapeDtypeStruct(values.shape, F32),...  53 us
    unnamed x1, local copies, waits for them, and re-layouts  1.67 us

profile of v2, /device:TPU:1, one launch (start us, length us, event | category | flops | bytes accessed | tf_op | source)
XLA Modules:
  0.0 54.7 jit_solution(7947161892240140602)
XLA Ops:
  0.0 53.0 %shard_map.73 = f32[2,16,16,128]{3,2,1,0:T(8,128)} custom-call(f32[2,16,16,128]{3,2,1,0:T(8,128)} %bitcast.5, bf16[2,128,128]{2,1,0:T(8,128)(2,1)} %constant.6.clone.hx_ref, bf16[2,256,256]{2,1,0:T(8,128)(2,1)} %constant.7.clone.h_ref, bf16[2,256,256]{2,1,0:T(8,128)(2,1)} %constant.8.clone.hb_ref, f32[128]{0:T(128)} %sx_ref.1, f32[1,256]{1,0:T(1,128)} %bitcast.6, ...), custom_call_target="tpu_custom_call" | custom-call | tf_op jit(solution)/shard_map/pallas_call | solution.py:155
  53.0 1.7 %copy.9 = f32[2,128,16,16]{1,3,2,0:T(8,128)} copy(f32[2,128,16,16]{1,3,2,0:T(8,128)} %bitcast.4) | data formatting | bytes 524288

commit v3 on v2

--- a/solution.py
+++ b/solution.py
@@ -48,20 +48,29 @@
     return pltpu.roll(tiles, 0, 2, stride=16, stride_axis=1)
 
 
-def kernel(a_ref, hx_ref, h_ref, hb_ref, sx_ref, sy_ref, sz_ref, out_ref,
+def kernel(a_ref, hx_ref, h_ref, hb_ref, hc_ref, sx_ref, sy_ref, sz_ref, out_ref,
            send1, recv1, recv2, send3, recv3, recv4, send_sem, recv_sem, own_sem):
     r, c = lax.axis_index("row"), lax.axis_index("col")
+    a = r % 8 * 2 + c % 2
+    b = r // 8 * 8 + c // 2
+
+    def at_a(t):
+        return {"row": b // 8 * 8 + t // 2, "col": b % 8 * 2 + t % 2}
+
+    def at_b(t):
+        return {"row": t // 8 * 8 + a // 2, "col": t % 8 * 2 + a % 2}
+
     barrier = pltpu.get_barrier_semaphore()
 
     @pl.loop(1, 16)
     def _(i):
-        pl.semaphore_signal(barrier, inc=1, device_id={"row": (r + i) % 16}, device_id_type=MESH)
-        pl.semaphore_signal(barrier, inc=1, device_id={"col": (c + i) % 16}, device_id_type=MESH)
+        pl.semaphore_signal(barrier, inc=1, device_id=at_a((a + i) % 16), device_id_type=MESH)
+        pl.semaphore_signal(barrier, inc=1, device_id=at_b((b + i) % 16), device_id_type=MESH)
 
     def slot(col):
         return col // 8 * 8 + (8 - col % 8) % 8
 
-    half = r // 8
+    half = a // 8
     near, far = half * 8, (1 - half) * 8
 
     def refs(k, h, base, mine, t):
@@ -74,19 +83,19 @@
         return recv3.at[h, t], recv4.at[h, mine]
 
     def own(k, h, side):
-        return pltpu.make_async_copy(*refs(k, h, (near, far)[side], *((r, r) if k in (0, 3) else (c, c))),
+        return pltpu.make_async_copy(*refs(k, h, (near, far)[side], *((a, a) if k in (0, 3) else (b, b))),
                                      own_sem.at[k, side, h])
 
     def start(k, side, h):
         base, rows = (near, far)[side], k in (0, 3)
-        axis, mine = ("row", r) if rows else ("col", c)
+        mine, at = (a, at_a) if rows else (b, at_b)
 
         @pl.loop(0 if rows and side else 1, 8 if rows else 16)
         def _(i):
-            t = base + (r + i) % 8 if rows else (c + i) % 16
+            t = base + (a + i) % 8 if rows else (b + i) % 16
             src, dst = refs(k, h, base, mine, t)
             pltpu.make_async_remote_copy(src, dst, send_sem.at[k, side, h], recv_sem.at[k, side, h],
-                                         device_id={axis: t}, device_id_type=MESH).start()
+                                         device_id=at(t), device_id_type=MESH).start()
         if not (rows and side):
             own(k, h, side).start()
 
@@ -102,6 +111,7 @@
     hx = hx_ref[0], hx_ref[1]
     table = h_ref[0], h_ref[1]
     backwards = hb_ref[0], hb_ref[1]
+    columns = hc_ref[0], hc_ref[1]
     for f in range(2):
         for h in range(2):
             rows = split(a_ref[f, pl.ds(8 * h, 8)].reshape(128, 128))
@@ -111,7 +121,7 @@
         start(0, side, h)
 
     symbol_y = jnp.broadcast_to(sy_ref[...], (256, 256)).T
-    symbol = sx_ref[r % 8 * 16 + c] + symbol_y + sz_ref[...]
+    symbol = sx_ref[a % 8 * 16 + b] + symbol_y + sz_ref[...]
     scale = lax.rsqrt(symbol)
 
     for side, h in OUT_NEXT:
@@ -120,16 +130,19 @@
     for side, h in OUT_NEXT:
         finish(1, side, h)
 
-    tiles = exchanged(recv2[...].reshape(64, 8, 128)).reshape(2, 16, 2, 8, 128)
+    tiles = exchanged(recv2[...].reshape(64, 8, 128)).reshape(2, 8, 2, 2, 8, 128)
     plane = jnp.concatenate(
-        [jnp.stack([tiles[0, :, g], tiles[1, :, g]], axis=1).reshape(256, 128) for g in range(2)], axis=1
+        [jnp.stack([jnp.stack([tiles[h, :, g, y] for h in range(2)], axis=1) for y in range(2)]).reshape(256, 128)
+         for g in range(2)], axis=1
     )
-    plane = dot(split(plane), table, NN)
+    plane = dot(split(plane), columns, NN)
     plane = dot(backwards, split(plane), NN) * scale
     plane = dot(table, split(plane), NN)
-    plane = dot(split(plane), table, NN).reshape(16, 2, 8, 256)
+    plane = dot(split(plane), columns, NT).reshape(2, 8, 2, 8, 256)
     for h in range(2):
-        part = jnp.stack([plane[:, h, :, :128], plane[:, h, :, 128:]], axis=1).reshape(32, 8, 128)
+        part = jnp.stack(
+            [jnp.stack([plane[y, :, h, :, 128 * g:128 * (g + 1)] for y in range(2)], axis=1) for g in range(2)], axis=1
+        ).reshape(32, 8, 128)
         send3[h] = exchanged(part).reshape(16, 16, 128)
     for side, h in BACK:
         start(2, side, h)
@@ -151,15 +164,17 @@
     vmem, smem = pl.BlockSpec(memory_space=pltpu.VMEM), pl.BlockSpec(memory_space=pltpu.SMEM)
     table, place = mode_table(256), np.arange(256)
     backwards = place // 8 * 8 + -place % 8
+    apart = (place % 128 // 16 * 2 + place // 128) * 16 + place % 16
     block = pltpu.VMEM((2, 16, 16, 128), F32)
     out = pl.pallas_call(
         kernel,
         out_shape=jax.ShapeDtypeStruct(values.shape, F32),
-        in_specs=[vmem, vmem, vmem, vmem, smem, vmem, vmem],
+        in_specs=[vmem, vmem, vmem, vmem, vmem, smem, vmem, vmem],
         out_specs=vmem,
         scratch_shapes=[block] * 6 + [pltpu.SemaphoreType.DMA((4, 2, 2))] * 3,
         compiler_params=pltpu.CompilerParams(collective_id=0, has_side_effects=True),
     )(values, jnp.asarray(mode_table(128)), jnp.asarray(table), jnp.asarray(table[:, :, backwards]),
+      jnp.asarray(table[:, apart]),
       symbol_x, symbol_y.reshape(1, 256), symbol_z.reshape(1, 256))
     return jnp.transpose(out, (0, 3, 1, 2))
 

time: 54.8 us -> 53.7 us (0.980)
  Pallas kernels: 53 us -> 51.8 us
    pallas_call x1, Pallas kernels: 53 us -> 51.8 us  [shards(): pl.pallas_call(kernel, out_shape=jax.ShapeDtypeStruct(values.shape, F32),...]
where the time goes in v3:
time: 53.7 us; the launch traced here: 53.5 us
  Pallas kernels  51.8 us (96%)
  local copies, waits for them, and re-layouts  1.67 us (3%)
    pallas_call x1, Pallas kernels, shards(): pl.pallas_call(kernel, out_shape=jax.ShapeDtypeStruct(values.shape, F32),...  51.8 us
    unnamed x1, local copies, waits for them, and re-layouts  1.67 us

profile of v3, /device:TPU:1, one launch (start us, length us, event | category | flops | bytes accessed | tf_op | source)
XLA Modules:
  0.0 53.5 jit_solution(12900247905751855441)
XLA Ops:
  0.0 51.8 %shard_map.82 = f32[2,16,16,128]{3,2,1,0:T(8,128)} custom-call(f32[2,16,16,128]{3,2,1,0:T(8,128)} %bitcast.5, bf16[2,128,128]{2,1,0:T(8,128)(2,1)} %constant.8.clone.hx_ref, bf16[2,256,256]{2,1,0:T(8,128)(2,1)} %constant.9.clone.h_ref, bf16[2,256,256]{2,1,0:T(8,128)(2,1)} %constant.10.clone.hb_ref, bf16[2,256,256]{2,1,0:T(8,128)(2,1)} %constant.11.clone.hc_ref, ...), custom_call_target="tpu_custom_call" | custom-call | tf_op jit(solution)/shard_map/pallas_call | solution.py:169
  51.8 1.7 %copy.10 = f32[2,128,16,16]{1,3,2,0:T(8,128)} copy(f32[2,128,16,16]{1,3,2,0:T(8,128)} %bitcast.4) | data formatting | bytes 524288

commit v4 on v3

--- a/solution.py
+++ b/solution.py
@@ -9,9 +9,9 @@
 from jax.sharding import PartitionSpec as P
 
 MESH = pl.DeviceIdType.MESH
-OUT = (1, 0), (0, 0), (0, 1), (1, 1)
-OUT_NEXT = (0, 0), (0, 1), (1, 0), (1, 1)
-BACK = (1, 0), (1, 1), (0, 0), (0, 1)
+OUT = (0, 0), (1, 0)
+OUT_NEXT = (0, 0), (1, 0)
+BACK = (1, 0), (0, 0)
 F32, BF16 = jnp.float32, jnp.bfloat16
 
 
@@ -75,12 +75,12 @@
 
     def refs(k, h, base, mine, t):
         if k == 0:
-            return send1.at[h, t], recv1.at[h, mine]
+            return send1.at[:, t], recv1.at[:, mine]
         if k == 1:
-            return recv1.at[h, pl.ds(base, 8), pl.ds(t, 1)], recv2.at[h, pl.ds(base, 8), pl.ds(mine, 1)]
+            return recv1.at[:, pl.ds(base, 8), pl.ds(t, 1)], recv2.at[:, pl.ds(base, 8), pl.ds(mine, 1)]
         if k == 2:
-            return send3.at[h, pl.ds(base, 8), pl.ds(slot(t), 1)], recv3.at[h, pl.ds(base, 8), pl.ds(mine, 1)]
-        return recv3.at[h, t], recv4.at[h, mine]
+            return send3.at[:, pl.ds(base, 8), pl.ds(slot(t), 1)], recv3.at[:, pl.ds(base, 8), pl.ds(mine, 1)]
+        return recv3.at[:, t], recv4.at[:, mine]
 
     def own(k, h, side):
         return pltpu.make_async_copy(*refs(k, h, (near, far)[side], *((a, a) if k in (0, 3) else (b, b))),
@@ -100,7 +100,7 @@
             own(k, h, side).start()
 
     def await_all(k, side, h, sem):
-        part = send1.at[h, pl.ds(0, 7 + side)] if k in (0, 3) else send1.at[h, pl.ds(0, 15), pl.ds(0, 8)]
+        part = send1.at[:, pl.ds(0, 7 + side)] if k in (0, 3) else send1.at[:, pl.ds(0, 15), pl.ds(0, 8)]
         pltpu.make_async_copy(part, part, sem.at[k, side, h]).wait()
 
     def finish(k, side, h):
@@ -152,8 +152,9 @@
     for side, h in BACK:
         finish(3, side, h)
         f = (half, 1 - half)[side]
-        rows = split(recv4[h, pl.ds(8 * f, 8)].reshape(128, 128))
-        out_ref[f, pl.ds(8 * h, 8)] = dot(rows, hx, TN).reshape(8, 16, 128)
+        for h in range(2):
+            rows = split(recv4[h, pl.ds(8 * f, 8)].reshape(128, 128))
+            out_ref[f, pl.ds(8 * h, 8)] = dot(rows, hx, TN).reshape(8, 16, 128)
     for k in range(4):
         for side, h in OUT:
             await_all(k, side, h, send_sem)

time: 53.7 us -> 53.1 us (0.989)
    pallas_call x1, Pallas kernels: 51.8 us -> 51.3 us  [shards(): pl.pallas_call(kernel, out_shape=jax.ShapeDtypeStruct(values.shape, F32),...]
where the time goes in v4:
time: 53.1 us; the launch traced here: 52.9 us
  Pallas kernels  51.3 us (97%)
  local copies, waits for them, and re-layouts  1.67 us (3%)
    pallas_call x1, Pallas kernels, shards(): pl.pallas_call(kernel, out_shape=jax.ShapeDtypeStruct(values.shape, F32),...  51.3 us
    unnamed x1, local copies, waits for them, and re-layouts  1.67 us

profile of v4, /device:TPU:1, one launch (start us, length us, event | category | flops | bytes accessed | tf_op | source)
XLA Modules:
  0.0 52.9 jit_solution(12127992800176836371)
XLA Ops:
  0.0 51.3 %shard_map.82 = f32[2,16,16,128]{3,2,1,0:T(8,128)} custom-call(f32[2,16,16,128]{3,2,1,0:T(8,128)} %bitcast.5, bf16[2,128,128]{2,1,0:T(8,128)(2,1)} %constant.8.clone.hx_ref, bf16[2,256,256]{2,1,0:T(8,128)(2,1)} %constant.9.clone.h_ref, bf16[2,256,256]{2,1,0:T(8,128)(2,1)} %constant.10.clone.hb_ref, bf16[2,256,256]{2,1,0:T(8,128)(2,1)} %constant.11.clone.hc_ref, ...), custom_call_target="tpu_custom_call" | custom-call | tf_op jit(solution)/shard_map/pallas_call | solution.py:170
  51.3 1.7 %copy.10 = f32[2,128,16,16]{1,3,2,0:T(8,128)} copy(f32[2,128,16,16]{1,3,2,0:T(8,128)} %bitcast.4) | data formatting | bytes 524288

commit v5 on v4

--- a/solution.py
+++ b/solution.py
@@ -90,9 +90,9 @@
         base, rows = (near, far)[side], k in (0, 3)
         mine, at = (a, at_a) if rows else (b, at_b)
 
-        @pl.loop(0 if rows and side else 1, 8 if rows else 16)
+        @pl.loop(0 if side or not rows else 1, 8 if rows else 15)
         def _(i):
-            t = base + (a + i) % 8 if rows else (b + i) % 16
+            t = base + (a + i) % 8 if rows else ((b // 8 + 1 + i % 2) % 2) * 8 + (b + 1 + i // 2) % 8
             src, dst = refs(k, h, base, mine, t)
             pltpu.make_async_remote_copy(src, dst, send_sem.at[k, side, h], recv_sem.at[k, side, h],
                                          device_id=at(t), device_id_type=MESH).start()

time: 53.1 us -> 52.9 us (level)
  no operation moved by 1% of the time
where the time goes in v5:
time: 52.9 us; the launch traced here: 52.7 us
  Pallas kernels  51.1 us (97%)
  local copies, waits for them, and re-layouts  1.67 us (3%)
    pallas_call x1, Pallas kernels, shards(): pl.pallas_call(kernel, out_shape=jax.ShapeDtypeStruct(values.shape, F32),...  51.1 us
    unnamed x1, local copies, waits for them, and re-layouts  1.67 us

profile of v5, /device:TPU:1, one launch (start us, length us, event | category | flops | bytes accessed | tf_op | source)
XLA Modules:
  0.0 52.7 jit_solution(17545784586889701822)
XLA Ops:
  0.0 51.1 %shard_map.82 = f32[2,16,16,128]{3,2,1,0:T(8,128)} custom-call(f32[2,16,16,128]{3,2,1,0:T(8,128)} %bitcast.5, bf16[2,128,128]{2,1,0:T(8,128)(2,1)} %constant.8.clone.hx_ref, bf16[2,256,256]{2,1,0:T(8,128)(2,1)} %constant.9.clone.h_ref, bf16[2,256,256]{2,1,0:T(8,128)(2,1)} %constant.10.clone.hb_ref, bf16[2,256,256]{2,1,0:T(8,128)(2,1)} %constant.11.clone.hc_ref, ...), custom_call_target="tpu_custom_call" | custom-call | tf_op jit(solution)/shard_map/pallas_call | solution.py:170
  51.1 1.7 %copy.10 = f32[2,128,16,16]{1,3,2,0:T(8,128)} copy(f32[2,128,16,16]{1,3,2,0:T(8,128)} %bitcast.4) | data formatting | bytes 524288
